TPU v7x, 32 devices: a whole 2x2x4 slice. The times are simulated.
32 devices in a mesh: grp: 2 (over x), rep: 8 (over z, y), blk: 2 (over core).
Axes of the slice: x: 2, y: 2, z: 4, core: 2. Of those that a mesh axis runs over, the one named last changes fastest.
Arguments:
- factors: float32 [16, 1280, 1280], P('grp', ('blk', 'rep')), as said below
- damping: float32 [16], P('grp'), may hold values from 0.1 to 1
Outputs:
- root: float32 [16, 1280, 1280], P('grp', ('blk', 'rep'))
- inv_root: float32 [16, 1280, 1280], P('grp', ('blk', 'rep'))
Inputs may be any that keep to these rules, and one draw needn't show every extreme that they name: `factors`: every factor is symmetric positive semidefinite.
All inputs are finite; a program needn't handle non-finite values.
Results may differ from a plain program's by a relative error of at most 0.0035.
The roundings to bfloat16 on the way count: a program that leaves them out, or rounds other values in their place, can miss the bound.
Values may be sent and summed in bfloat16 or wider, within the bound.
No kernel may reach another device: no remote copies, remote signals or barrier semaphores. Data moves between devices by JAX's collectives and lax.ppermute only.
A program may use at most 128 MiB of HBM per device.

v0:
```python
import jax
import jax.numpy as jnp
from jax import lax
from jax.sharding import PartitionSpec as P

ITERS = 4


def per_device(factors, damping):
    fac_grp = factors.shape[0]
    row_count = factors.shape[1]
    order_full = factors.shape[2]
    rep_count = lax.axis_size("rep")
    fac_rep = fac_grp // rep_count
    blk_rows = row_count * rep_count
    blk_idx = lax.axis_index("blk")
    rep_idx = lax.axis_index("rep")
    row_ids = blk_idx * blk_rows + rep_idx * row_count + lax.iota(jnp.int32, row_count)
    col_ids = lax.iota(jnp.int32, order_full)
    eye_block = (row_ids[:, None] == col_ids[None, :]).astype(jnp.float32)
    damped = factors + damping[:, None, None] * eye_block[None, :, :]
    factor_norms = jnp.sqrt(lax.psum(jnp.sum(damped * damped, axis=(1, 2)), ("rep", "blk")))
    own_rows = lax.all_to_all(damped, "rep", split_axis=0, concat_axis=1, tiled=True)
    own_norms = lax.dynamic_slice_in_dim(factor_norms, rep_idx * fac_rep, fac_rep)
    iterate = (own_rows / own_norms[:, None, None]).astype(jnp.bfloat16)
    iter_rows = blk_idx * blk_rows + lax.iota(jnp.int32, blk_rows)
    eye_rows = (iter_rows[:, None] == col_ids[None, :]).astype(jnp.float32)
    inverse = eye_rows[None, :, :].astype(jnp.bfloat16)
    for sweep_idx in range(ITERS):
        whole_iter, whole_inv = (
            lax.all_gather(iterate, "blk", axis=1, tiled=True),
            lax.all_gather(inverse, "blk", axis=1, tiled=True),
        )
        eye_full = jnp.eye(order_full, dtype=jnp.float32)
        moment_full = jnp.einsum(
            "fik,fkj->fij", whole_inv, whole_iter, preferred_element_type=jnp.float32
        )
        step_full = ((3.0 * eye_full[None, :, :] - moment_full) * 0.5).astype(jnp.bfloat16)
        step_rows = lax.dynamic_slice_in_dim(step_full, blk_idx * blk_rows, blk_rows, 1)
        new_iterate = jnp.einsum(
            "fik,fkj->fij", iterate, step_full, preferred_element_type=jnp.float32
        )
        new_inverse = jnp.einsum(
            "fik,fkj->fij", step_rows, whole_inv, preferred_element_type=jnp.float32
        )
        iterate = new_iterate.astype(jnp.bfloat16)
        inverse = new_inverse.astype(jnp.bfloat16)
    root_block, inv_block = (
        lax.all_to_all(iterate, "rep", split_axis=1, concat_axis=0, tiled=True),
        lax.all_to_all(inverse, "rep", split_axis=1, concat_axis=0, tiled=True),
    )
    root_scale = jnp.sqrt(factor_norms)[:, None, None]
    return (root_block.astype(jnp.float32) * root_scale, inv_block.astype(jnp.float32) / root_scale)


def solution(mesh):
    return jax.shard_map(
        per_device,
        mesh=mesh,
        in_specs=(P("grp", ("blk", "rep"), None), P("grp")),
        out_specs=(P("grp", ("blk", "rep"), None), P("grp", ("blk", "rep"), None)),
        check_vma=False,
    )
```

profile of v0, /device:TPU:0, one launch (start us, length us, event | category | flops | bytes accessed | tf_op | source)
XLA Modules:
  0.0 384.2 jit_solution(16059342983351797581)
XLA Ops:
  7.2 0.1 fusion.21
  7.3 4.3 %multiply_reduce_fusion = (f32[8]{0:T(128)S(1)}, f32[8,80,1280]{2,1,0:T(8,128)}) fusion(f32[8,80,1280]{2,1,0:T(8,128)} %param.2, f32[80,1280]{1,0:T(8,128)S(1)} %fusion.21, f32[8]{0:T(128)} %param.3), kind=kLoop, calls=%fused_computation.20 | loop fusion | flops 3276792 | bytes 6963264 | tf_op jit(solution)/shard_map/reduce_sum | solution.py:22
  11.6 7.3 %all-to-all-start = ((f32[8,80,1280]{2,1,0:T(8,128)}), f32[8,80,1280]{2,1,0:T(8,128)S(1)}, u32[]{:S(2)}, u32[]{:S(2)}) async-start(f32[8,80,1280]{2,1,0:T(8,128)} %get-tuple-element.3), calls=%async_computation | async-start | bytes 6553600 | tf_op jit(solution)/shard_map/all_to_all | solution.py:23
  19.0 1.5 convert_convert_fusion
  20.5 80.0 %psum.7 = f32[8]{0:T(128)S(1)} all-reduce(f32[8]{0:T(128)S(1)} %get-tuple-element.2), channel_id=1, replica_groups=mesh['grp'=2,'rep'=8,'blk'=2] {'rep','blk'}, use_global_device_ids=true, to_apply=%region_1.0 | all-reduce | flops 8 | bytes 64 | tf_op jit(solution)/shard_map/psum | solution.py:22
  100.6 0.6 dynamic_slice.2
  101.2 2.0 divide_convert_fusion
  103.3 20.4 %all-gather.17.cloned.1.call-done = bf16[1,1280,1280]{2,1,0:T(8,128)(2,1)} async-done(((bf16[1,640,1280]{2,1,0:T(8,128)(2,1)}), bf16[1,1280,1280]{2,1,0:T(8,128)(2,1)}) %all-gather.17.cloned.1.call-update) | async-done | bytes 3276816 | tf_op jit(solution)/shard_map/all_gather | solution.py:31
  123.7 7.3 %fusion.4 = bf16[1280,1280]{1,0:T(8,128)(2,1)S(1)} fusion(bf16[1,1280,1280]{2,1,0:T(8,128)(2,1)} %all-gather.17.cloned.1.call-done, bf16[1,1280,1280]{2,1,0:T(8,128)(2,1)} %all-gather.15.cloned.1.call-done), kind=kOutput, calls=%fused_computation.8 | convolution fusion | flops 4202496000 | bytes 9830400 | tf_op jit(solution)/shard_map/fik,fkj->fij/dot_general | solution.py:35
  131.1 1.7 copy-done.5
  132.8 3.5 convolution_convert_fusion.6
  136.3 0.0 all-gather.19.cloned.1.call-start
  136.4 5.9 %fusion.12 = bf16[640,1280]{1,0:T(8,128)(2,1)} fusion(bf16[1,1280,1280]{2,1,0:T(8,128)(2,1)} %all-gather.15.cloned.1.call-done, bf16[1280,1280]{1,0:T(8,128)(2,1)} %copy-done.5, s32[]{:T(128)S(6)} %select_n.10), kind=kOutput, calls=%fused_computation.22 | convolution fusion | flops 2097971200 | bytes 6553604 | tf_op jit(solution)/shard_map/fik,fkj->fij/dot_general | solution.py:43
  142.3 0.2 all-gather.25.cloned.1.call-start
  142.5 7.5 %all-gather.21.cloned.1.call-done = bf16[1280,1280]{1,0:T(8,128)(2,1)} async-done(((bf16[640,1280]{1,0:T(8,128)(2,1)}), bf16[1280,1280]{1,0:T(8,128)(2,1)}) %all-gather.21.cloned.1.call-update) | async-done | bytes 3276816 | tf_op jit(solution)/shard_map/all_gather | solution.py:31
  150.0 15.5 %all-gather.19.cloned.1.call-done = bf16[1280,1280]{1,0:T(8,128)(2,1)} async-done(((bf16[640,1280]{1,0:T(8,128)(2,1)}), bf16[1280,1280]{1,0:T(8,128)(2,1)}) %all-gather.19.cloned.1.call-update) | async-done | bytes 3276816 | tf_op jit(solution)/shard_map/all_gather | solution.py:32
  165.5 7.3 %fusion.5 = bf16[1280,1280]{1,0:T(8,128)(2,1)S(1)} fusion(bf16[1280,1280]{1,0:T(8,128)(2,1)} %all-gather.19.cloned.1.call-done, bf16[1280,1280]{1,0:T(8,128)(2,1)} %all-gather.21.cloned.1.call-done), kind=kOutput, calls=%fused_computation.9 | convolution fusion | flops 4202496000 | bytes 9830400 | tf_op jit(solution)/shard_map/fik,fkj->fij/dot_general | solution.py:35
  172.8 1.7 copy-done.7
  174.5 3.5 convolution_convert_fusion.5
  178.1 5.9 %convolution_convert_fusion.4 = bf16[640,1280]{1,0:T(8,128)(2,1)} fusion(bf16[1280,1280]{1,0:T(8,128)(2,1)} %all-gather.19.cloned.1.call-done, bf16[1280,1280]{1,0:T(8,128)(2,1)} %copy-done.7, s32[]{:T(128)S(6)} %select_n.10), kind=kOutput, calls=%fused_computation.27 | convolution fusion | flops 2097971200 | bytes 6553604 | tf_op jit(solution)/shard_map/fik,fkj->fij/dot_general | solution.py:43
  184.1 7.6 %all-gather.25.cloned.1.call-done = bf16[1280,1280]{1,0:T(8,128)(2,1)} async-done(((bf16[640,1280]{1,0:T(8,128)(2,1)}), bf16[1280,1280]{1,0:T(8,128)(2,1)}) %all-gather.25.cloned.1.call-update) | async-done | bytes 3276816 | tf_op jit(solution)/shard_map/all_gather | solution.py:31
  191.7 15.5 %all-gather.23.cloned.1.call-done = bf16[1280,1280]{1,0:T(8,128)(2,1)} async-done(((bf16[640,1280]{1,0:T(8,128)(2,1)}), bf16[1280,1280]{1,0:T(8,128)(2,1)}) %all-gather.23.cloned.1.call-update) | async-done | bytes 3276816 | tf_op jit(solution)/shard_map/all_gather | solution.py:32
  207.2 7.3 %fusion.6 = bf16[1280,1280]{1,0:T(8,128)(2,1)S(1)} fusion(bf16[1280,1280]{1,0:T(8,128)(2,1)} %all-gather.23.cloned.1.call-done, bf16[1280,1280]{1,0:T(8,128)(2,1)} %all-gather.25.cloned.1.call-done), kind=kOutput, calls=%fused_computation.10 | convolution fusion | flops 4202496000 | bytes 9830400 | tf_op jit(solution)/shard_map/fik,fkj->fij/dot_general | solution.py:35
  214.6 1.7 copy-done.8
  216.3 3.5 convolution_convert_fusion.3
  219.8 0.3 all-gather.27.cloned.1.call-start
  220.1 5.9 %convolution_convert_fusion.2 = bf16[640,1280]{1,0:T(8,128)(2,1)} fusion(bf16[1280,1280]{1,0:T(8,128)(2,1)} %all-gather.23.cloned.1.call-done, bf16[1280,1280]{1,0:T(8,128)(2,1)} %copy-done.8, s32[]{:T(128)S(6)} %select_n.10), kind=kOutput, calls=%fused_computation.25 | convolution fusion | flops 2097971200 | bytes 6553604 | tf_op jit(solution)/shard_map/fik,fkj->fij/dot_general | solution.py:43
  226.0 7.5 %all-gather.29.cloned.1.call-done = bf16[1280,1280]{1,0:T(8,128)(2,1)} async-done(((bf16[640,1280]{1,0:T(8,128)(2,1)}), bf16[1280,1280]{1,0:T(8,128)(2,1)}) %all-gather.29.cloned.1.call-update) | async-done | bytes 3276816 | tf_op jit(solution)/shard_map/all_gather | solution.py:31
  233.4 15.6 %all-gather.27.cloned.1.call-done = bf16[1280,1280]{1,0:T(8,128)(2,1)} async-done(((bf16[640,1280]{1,0:T(8,128)(2,1)}), bf16[1280,1280]{1,0:T(8,128)(2,1)}) %all-gather.27.cloned.1.call-update) | async-done | bytes 3276816 | tf_op jit(solution)/shard_map/all_gather | solution.py:32
  249.1 7.3 %fusion.7 = bf16[1280,1280]{1,0:T(8,128)(2,1)S(1)} fusion(bf16[1280,1280]{1,0:T(8,128)(2,1)} %all-gather.27.cloned.1.call-done, bf16[1280,1280]{1,0:T(8,128)(2,1)} %all-gather.29.cloned.1.call-done), kind=kOutput, calls=%fused_computation.11 | convolution fusion | flops 4202496000 | bytes 9830400 | tf_op jit(solution)/shard_map/fik,fkj->fij/dot_general | solution.py:35
  256.4 2.3 fusion.15
  258.7 2.5 copy.11
  261.3 0.6 broadcast.81
  261.9 12.2 %reduce.1 = bf16[640,1280]{1,0:T(8,128)(2,1)} reduce(bf16[640,1,1280]{2,1,0:T(2,128)(2,1)S(1)} %bitcast.46, bf16[]{:T(256)} %broadcast.81), dimensions={1}, to_apply=%bitcast.43.reduce_sub_computation | reduce | bytes 3276802
  274.1 3.9 %reshape.220 = bf16[8,2,51200]{2,1,0:T(2,128)(2,1)} reshape(bf16[640,1280]{1,0:T(8,128)(2,1)} %reduce.1) | data formatting | bytes 3276800
  278.0 5.9 %all-to-all-start.1 = ((bf16[8,2,51200]{2,1,0:T(2,128)(2,1)}), bf16[8,2,51200]{2,1,0:T(2,128)(2,1)}, u32[]{:S(2)}, u32[]{:S(2)}) async-start(bf16[8,2,51200]{2,1,0:T(2,128)(2,1)} %reshape.220), calls=%async_computation.1 | async-start | bytes 3276800 | tf_op jit(solution)/shard_map/all_to_all | solution.py:49
  284.0 3.7 fusion.16
  287.7 2.5 copy.10
  290.3 12.1 %reduce = bf16[640,1280]{1,0:T(8,128)(2,1)} reduce(bf16[640,1,1280]{2,1,0:T(2,128)(2,1)S(1)} %bitcast.47, bf16[]{:T(256)} %broadcast.81), dimensions={1}, to_apply=%bitcast.42.reduce_sub_computation | reduce | bytes 3276802
  302.3 3.7 reshape.222
  306.0 16.8 %all-to-all-done.1 = bf16[8,2,51200]{2,1,0:T(2,128)(2,1)} async-done(((bf16[8,2,51200]{2,1,0:T(2,128)(2,1)}), bf16[8,2,51200]{2,1,0:T(2,128)(2,1)}, u32[]{:S(2)}, u32[]{:S(2)}) %all-to-all-start.1) | async-done | bytes 1638432 | tf_op jit(solution)/shard_map/all_to_all | solution.py:49
  322.8 4.3 %all-to-all-start.2 = ((bf16[8,2,51200]{2,1,0:T(2,128)(2,1)}), bf16[8,2,51200]{2,1,0:T(2,128)(2,1)}, u32[]{:S(2)}, u32[]{:S(2)}) async-start(bf16[8,2,51200]{2,1,0:T(2,128)(2,1)} %reshape.222), calls=%async_computation.2 | async-start | bytes 3276800 | tf_op jit(solution)/shard_map/all_to_all | solution.py:50
  327.1 6.4 %reshape.221 = bf16[640,1,1280]{2,1,0:T(2,128)(2,1)} reshape(bf16[8,2,51200]{2,1,0:T(2,128)(2,1)} %all-to-all-done.1) | data formatting | bytes 3276800
  333.5 2.1 copy.6
  335.6 29.5 %all-to-all-done.2 = bf16[8,2,51200]{2,1,0:T(2,128)(2,1)} async-done(((bf16[8,2,51200]{2,1,0:T(2,128)(2,1)}), bf16[8,2,51200]{2,1,0:T(2,128)(2,1)}, u32[]{:S(2)}, u32[]{:S(2)}) %all-to-all-start.2) | async-done | bytes 1638432 | tf_op jit(solution)/shard_map/all_to_all | solution.py:50
  365.1 6.4 %reshape.223 = bf16[640,1,1280]{2,1,0:T(2,128)(2,1)} reshape(bf16[8,2,51200]{2,1,0:T(2,128)(2,1)} %all-to-all-done.2) | data formatting | bytes 3276800
  371.5 2.1 copy.7
  373.6 3.5 broadcast_divide_fusion
  (33 shorter events, 0.4 us)
Async XLA Ops:
  11.6 89.6 %all-to-all-start = ((f32[8,80,1280]{2,1,0:T(8,128)}), f32[8,80,1280]{2,1,0:T(8,128)S(1)}, u32[]{:S(2)}, u32[]{:S(2)}) async-start(f32[8,80,1280]{2,1,0:T(8,128)} %get-tuple-element.3), calls=%async_computation | async-start | bytes 6553600 | tf_op jit(solution)/shard_map/all_to_all | solution.py:23
  18.9 84.4 %all-gather.15.cloned.1.call-start = ((), (), s32[]{:S(2)}) async-start(), calls=%async_computation.3 | async-start | bytes 4915200 | tf_op jit(solution)/shard_map/all_gather | solution.py:32
  20.5 103.3 %all-gather.17.cloned.1.call-start = ((), (), s32[]{:S(2)}) async-start(), calls=%async_computation.4 | async-start | bytes 4915200 | tf_op jit(solution)/shard_map/all_gather | solution.py:31
  103.2 29.6 %copy-start = (bf16[8,80,1280]{2,1,0:T(8,128)(2,1)S(1)}, bf16[8,80,1280]{2,1,0:T(8,128)(2,1)}, u32[]{:S(2)}) copy-start(bf16[8,80,1280]{2,1,0:T(8,128)(2,1)} %divide_convert_fusion) | copy-start | bytes 4915204
  103.2 46.7 %all-gather.21.cloned.1.call-start = ((), (), s32[]{:S(2)}) async-start(), calls=%async_computation.6 | async-start | bytes 4915200 | tf_op jit(solution)/shard_map/all_gather | solution.py:31
  131.1 1.7 copy-start.5
  136.3 29.1 %all-gather.19.cloned.1.call-start = ((), (), s32[]{:S(2)}) async-start(), calls=%async_computation.5 | async-start | bytes 4915200 | tf_op jit(solution)/shard_map/all_gather | solution.py:32
  142.3 32.2 %copy-start.1 = (bf16[640,1280]{1,0:T(8,128)(2,1)S(1)}, bf16[640,1280]{1,0:T(8,128)(2,1)}, u32[]{:S(2)}) copy-start(bf16[640,1280]{1,0:T(8,128)(2,1)} %convolution_convert_fusion.6) | copy-start | bytes 4915204
  142.3 49.4 %all-gather.25.cloned.1.call-start = ((), (), s32[]{:S(2)}) async-start(), calls=%async_computation.8 | async-start | bytes 4915200 | tf_op jit(solution)/shard_map/all_gather | solution.py:31
  172.8 1.7 copy-start.7
  178.1 29.1 %all-gather.23.cloned.1.call-start = ((), (), s32[]{:S(2)}) async-start(), calls=%async_computation.7 | async-start | bytes 4915200 | tf_op jit(solution)/shard_map/all_gather | solution.py:32
  184.0 32.2 %copy-start.2 = (bf16[640,1280]{1,0:T(8,128)(2,1)S(1)}, bf16[640,1280]{1,0:T(8,128)(2,1)}, u32[]{:S(2)}) copy-start(bf16[640,1280]{1,0:T(8,128)(2,1)} %convolution_convert_fusion.5) | copy-start | bytes 4915204
  184.0 49.4 %all-gather.29.cloned.1.call-start = ((), (), s32[]{:S(2)}) async-start(), calls=%async_computation.10 | async-start | bytes 4915200 | tf_op jit(solution)/shard_map/all_gather | solution.py:31
  214.5 1.7 copy-start.8
  219.8 29.3 %all-gather.27.cloned.1.call-start = ((), (), s32[]{:S(2)}) async-start(), calls=%async_computation.9 | async-start | bytes 4915200 | tf_op jit(solution)/shard_map/all_gather | solution.py:32
  226.0 30.5 %copy-start.3 = (bf16[640,1280]{1,0:T(8,128)(2,1)S(1)}, bf16[640,1280]{1,0:T(8,128)(2,1)}, u32[]{:S(2)}) copy-start(bf16[640,1280]{1,0:T(8,128)(2,1)} %convolution_convert_fusion.3) | copy-start | bytes 4915204
  256.4 2.3 copy-start.6
  274.1 9.9 %copy-start.4 = (bf16[1280,1280]{1,0:T(8,128)(2,1)S(1)}, bf16[1280,1280]{1,0:T(8,128)(2,1)}, u32[]{:S(2)}) copy-start(bf16[1280,1280]{1,0:T(8,128)(2,1)} %all-gather.27.cloned.1.call-done) | copy-start | bytes 9830404
  278.0 44.7 %all-to-all-start.1 = ((bf16[8,2,51200]{2,1,0:T(2,128)(2,1)}), bf16[8,2,51200]{2,1,0:T(2,128)(2,1)}, u32[]{:S(2)}, u32[]{:S(2)}) async-start(bf16[8,2,51200]{2,1,0:T(2,128)(2,1)} %reshape.220), calls=%async_computation.1 | async-start | bytes 3276800 | tf_op jit(solution)/shard_map/all_to_all | solution.py:49
  322.8 42.3 %all-to-all-start.2 = ((bf16[8,2,51200]{2,1,0:T(2,128)(2,1)}), bf16[8,2,51200]{2,1,0:T(2,128)(2,1)}, u32[]{:S(2)}, u32[]{:S(2)}) async-start(bf16[8,2,51200]{2,1,0:T(2,128)(2,1)} %reshape.222), calls=%async_computation.2 | async-start | bytes 3276800 | tf_op jit(solution)/shard_map/all_to_all | solution.py:50
Sparse Core Ops, SparseCore 0:
  21.8 13.7 all-gather.14
  103.3 20.3 all-gather.16
  136.4 13.4 all-gather.20
  151.9 13.4 all-gather.18
  178.2 13.4 all-gather.24
  193.7 13.4 all-gather.22
  219.9 13.4 all-gather.28
  235.5 13.4 all-gather.26
where the time goes:
time: 391 us; the launch traced here: 384 us
  waiting for transfers between devices  136 us (35%)
  blocking collectives  80 us (20%)
  matrix products  63.5 us (16%)
  local copies, waits for them, and re-layouts  36.1 us (9%)
  other arithmetic  35.8 us (9%)
  starting transfers between devices  18.3 us (5%)
  between operations  14.6 us (4%)
    psum x1, blocking collectives, per_device(): lax.psum(jnp.sum(damped * damped, axis=(1, 2)), ('rep', 'blk'))  80 us
    all_gather x4, waiting for transfers between devices, per_device(): lax.all_gather(inverse, 'blk', axis=1, tiled=True)  46.7 us
    all_gather x4, waiting for transfers between devices, per_device(): lax.all_gather(iterate, 'blk', axis=1, tiled=True)  43 us
    unnamed x25, local copies, waits for them, and re-layouts  30.4 us
    all_to_all x1, waiting for transfers between devices, per_device(): lax.all_to_all(inverse, 'rep', split_axis=1, concat_axis=0, tiled=True)  29.5 us
    dot_general x4, matrix products, per_device(): jnp.einsum('fik,fkj->fij', whole_inv, whole_iter, preferred_element_type=...  29.3 us
    unnamed x2, other arithmetic  24.3 us
    dot_general x4, matrix products, per_device(): jnp.einsum('fik,fkj->fij', step_rows, whole_inv, preferred_element_type=j...  21.3 us
  transfers between devices with their start and end apart: 11, of which 9 were waited for; matrix products, arithmetic and copies ran while one was open for 14% of the time, Pallas kernels for 0%

commit v1 on v0

--- a/solution.py
+++ b/solution.py
@@ -1,9 +1,19 @@
+import functools
 import jax
 import jax.numpy as jnp
 from jax import lax
 from jax.sharding import PartitionSpec as P
 
 ITERS = 4
+
+
+def _cover_sizes(load, axis_id, axis_key):
+    for ix in (axis_id, axis_key):
+        load = lax.psum(load, axis_name=ix)
+    return load
+
+
+outputs_proceed = functools.partial(_cover_sizes, axis_id="blk", axis_key="rep")
 
 
 def per_device(factors, damping):
@@ -19,7 +29,7 @@
     col_ids = lax.iota(jnp.int32, order_full)
     eye_block = (row_ids[:, None] == col_ids[None, :]).astype(jnp.float32)
     damped = factors + damping[:, None, None] * eye_block[None, :, :]
-    factor_norms = jnp.sqrt(lax.psum(jnp.sum(damped * damped, axis=(1, 2)), ("rep", "blk")))
+    factor_norms = jnp.sqrt(outputs_proceed(jnp.sum(damped * damped, axis=(1, 2))))
     own_rows = lax.all_to_all(damped, "rep", split_axis=0, concat_axis=1, tiled=True)
     own_norms = lax.dynamic_slice_in_dim(factor_norms, rep_idx * fac_rep, fac_rep)
     iterate = (own_rows / own_norms[:, None, None]).astype(jnp.bfloat16)

time: 391 us -> 383 us (0.980)
  blocking collectives: 80 us -> 67.6 us
  waiting for transfers between devices: 136 us -> 140 us
    psum x1 -> x2, blocking collectives: 80 us -> 67.6 us  [_cover_sizes(): load = lax.psum(load, axis_name=ix)]
  transfers between devices with their start and end apart: 11 -> 11, of which waited for: 9 -> 10; matrix products, arithmetic and copies ran while one was open for 14% -> 14% of each run, Pallas kernels for 0% -> 0%
where the time goes in v1:
time: 383 us; the launch traced here: 375 us
  waiting for transfers between devices  140 us (37%)
  blocking collectives  67.6 us (18%)
  matrix products  63.4 us (17%)
  local copies, waits for them, and re-layouts  36 us (9%)
  other arithmetic  35.5 us (9%)
  starting transfers between devices  18.3 us (5%)
  between operations  14.6 us (4%)
    psum x2, blocking collectives, _cover_sizes(): load = lax.psum(load, axis_name=ix)  67.6 us
    all_gather x4, waiting for transfers between devices, per_device(): lax.all_gather(inverse, 'blk', axis=1, tiled=True)  46.7 us
    all_gather x4, waiting for transfers between devices, per_device(): lax.all_gather(iterate, 'blk', axis=1, tiled=True)  43 us
    unnamed x25, local copies, waits for them, and re-layouts  30.3 us
    all_to_all x1, waiting for transfers between devices, per_device(): lax.all_to_all(inverse, 'rep', split_axis=1, concat_axis=0, tiled=True)  29.5 us
    dot_general x4, matrix products, per_device(): jnp.einsum('fik,fkj->fij', whole_inv, whole_iter, preferred_element_type=...  29.3 us
    unnamed x2, other arithmetic  24 us
    dot_general x4, matrix products, per_device(): jnp.einsum('fik,fkj->fij', step_rows, whole_inv, preferred_element_type=j...  21.3 us
  transfers between devices with their start and end apart: 11, of which 10 were waited for; matrix products, arithmetic and copies ran while one was open for 14% of the time, Pallas kernels for 0%

profile of v1, /device:TPU:0, one launch (start us, length us, event | category | flops | bytes accessed | tf_op | source)
XLA Modules:
  0.0 375.3 jit_solution(17252381644066995238)
XLA Ops:
  7.3 4.3 %multiply_reduce_fusion = (f32[8]{0:T(128)S(1)}, f32[8,80,1280]{2,1,0:T(8,128)}) fusion(f32[8,80,1280]{2,1,0:T(8,128)} %param.2, f32[80,1280]{1,0:T(8,128)S(1)} %fusion.21, f32[8]{0:T(128)} %param.3), kind=kLoop, calls=%fused_computation.20 | loop fusion | flops 3276792 | bytes 6963264 | tf_op jit(solution)/shard_map/reduce_sum | solution.py:32
  11.6 7.3 %all-to-all-start = ((f32[8,80,1280]{2,1,0:T(8,128)}), f32[8,80,1280]{2,1,0:T(8,128)S(1)}, u32[]{:S(2)}, u32[]{:S(2)}) async-start(f32[8,80,1280]{2,1,0:T(8,128)} %get-tuple-element.3), calls=%async_computation | async-start | bytes 6553600 | tf_op jit(solution)/shard_map/all_to_all | solution.py:33
  19.0 1.5 convert_convert_fusion
  20.5 2.5 psum.14
  23.0 65.1 %psum.15 = f32[8]{0:T(128)S(1)} all-reduce(f32[8]{0:T(128)S(1)} %psum.14), channel_id=1, replica_groups=mesh['grp'=2,'rep'=8,'blk'=2] {'rep'}, use_global_device_ids=true, to_apply=%region_2.0 | all-reduce | flops 8 | bytes 64 | tf_op jit(solution)/shard_map/psum | solution.py:12
  88.1 0.7 dynamic_slice.2
  88.8 3.7 all-to-all-done
  92.5 2.1 divide_convert_fusion
  94.7 20.4 %all-gather.17.cloned.1.call-done = bf16[1,1280,1280]{2,1,0:T(8,128)(2,1)} async-done(((bf16[1,640,1280]{2,1,0:T(8,128)(2,1)}), bf16[1,1280,1280]{2,1,0:T(8,128)(2,1)}) %all-gather.17.cloned.1.call-update) | async-done | bytes 3276816 | tf_op jit(solution)/shard_map/all_gather | solution.py:41
  115.1 7.3 %fusion.4 = bf16[1280,1280]{1,0:T(8,128)(2,1)S(1)} fusion(bf16[1,1280,1280]{2,1,0:T(8,128)(2,1)} %all-gather.17.cloned.1.call-done, bf16[1,1280,1280]{2,1,0:T(8,128)(2,1)} %all-gather.15.cloned.1.call-done), kind=kOutput, calls=%fused_computation.8 | convolution fusion | flops 4202496000 | bytes 9830400 | tf_op jit(solution)/shard_map/fik,fkj->fij/dot_general | solution.py:45
  122.5 1.7 copy-done.5
  124.2 3.5 convolution_convert_fusion.6
  127.7 5.9 %fusion.12 = bf16[640,1280]{1,0:T(8,128)(2,1)} fusion(bf16[1,1280,1280]{2,1,0:T(8,128)(2,1)} %all-gather.15.cloned.1.call-done, bf16[1280,1280]{1,0:T(8,128)(2,1)} %copy-done.5, s32[]{:T(128)S(6)} %select_n.10), kind=kOutput, calls=%fused_computation.22 | convolution fusion | flops 2097971200 | bytes 6553604 | tf_op jit(solution)/shard_map/fik,fkj->fij/dot_general | solution.py:53
  133.6 0.2 all-gather.25.cloned.1.call-start
  133.8 7.5 %all-gather.21.cloned.1.call-done = bf16[1280,1280]{1,0:T(8,128)(2,1)} async-done(((bf16[640,1280]{1,0:T(8,128)(2,1)}), bf16[1280,1280]{1,0:T(8,128)(2,1)}) %all-gather.21.cloned.1.call-update) | async-done | bytes 3276816 | tf_op jit(solution)/shard_map/all_gather | solution.py:41
  141.3 15.5 %all-gather.19.cloned.1.call-done = bf16[1280,1280]{1,0:T(8,128)(2,1)} async-done(((bf16[640,1280]{1,0:T(8,128)(2,1)}), bf16[1280,1280]{1,0:T(8,128)(2,1)}) %all-gather.19.cloned.1.call-update) | async-done | bytes 3276816 | tf_op jit(solution)/shard_map/all_gather | solution.py:42
  156.8 7.3 %fusion.5 = bf16[1280,1280]{1,0:T(8,128)(2,1)S(1)} fusion(bf16[1280,1280]{1,0:T(8,128)(2,1)} %all-gather.19.cloned.1.call-done, bf16[1280,1280]{1,0:T(8,128)(2,1)} %all-gather.21.cloned.1.call-done), kind=kOutput, calls=%fused_computation.9 | convolution fusion | flops 4202496000 | bytes 9830400 | tf_op jit(solution)/shard_map/fik,fkj->fij/dot_general | solution.py:45
  164.2 1.7 copy-done.7
  165.9 3.5 convolution_convert_fusion.5
  169.4 5.9 %convolution_convert_fusion.4 = bf16[640,1280]{1,0:T(8,128)(2,1)} fusion(bf16[1280,1280]{1,0:T(8,128)(2,1)} %all-gather.19.cloned.1.call-done, bf16[1280,1280]{1,0:T(8,128)(2,1)} %copy-done.7, s32[]{:T(128)S(6)} %select_n.10), kind=kOutput, calls=%fused_computation.27 | convolution fusion | flops 2097971200 | bytes 6553604 | tf_op jit(solution)/shard_map/fik,fkj->fij/dot_general | solution.py:53
  175.4 7.6 %all-gather.25.cloned.1.call-done = bf16[1280,1280]{1,0:T(8,128)(2,1)} async-done(((bf16[640,1280]{1,0:T(8,128)(2,1)}), bf16[1280,1280]{1,0:T(8,128)(2,1)}) %all-gather.25.cloned.1.call-update) | async-done | bytes 3276816 | tf_op jit(solution)/shard_map/all_gather | solution.py:41
  183.0 15.5 %all-gather.23.cloned.1.call-done = bf16[1280,1280]{1,0:T(8,128)(2,1)} async-done(((bf16[640,1280]{1,0:T(8,128)(2,1)}), bf16[1280,1280]{1,0:T(8,128)(2,1)}) %all-gather.23.cloned.1.call-update) | async-done | bytes 3276816 | tf_op jit(solution)/shard_map/all_gather | solution.py:42
  198.5 7.3 %fusion.6 = bf16[1280,1280]{1,0:T(8,128)(2,1)S(1)} fusion(bf16[1280,1280]{1,0:T(8,128)(2,1)} %all-gather.23.cloned.1.call-done, bf16[1280,1280]{1,0:T(8,128)(2,1)} %all-gather.25.cloned.1.call-done), kind=kOutput, calls=%fused_computation.10 | convolution fusion | flops 4202496000 | bytes 9830400 | tf_op jit(solution)/shard_map/fik,fkj->fij/dot_general | solution.py:45
  205.9 1.7 copy-done.8
  207.6 3.5 convolution_convert_fusion.3
  211.1 0.3 all-gather.27.cloned.1.call-start
  211.3 5.9 %convolution_convert_fusion.2 = bf16[640,1280]{1,0:T(8,128)(2,1)} fusion(bf16[1280,1280]{1,0:T(8,128)(2,1)} %all-gather.23.cloned.1.call-done, bf16[1280,1280]{1,0:T(8,128)(2,1)} %copy-done.8, s32[]{:T(128)S(6)} %select_n.10), kind=kOutput, calls=%fused_computation.25 | convolution fusion | flops 2097971200 | bytes 6553604 | tf_op jit(solution)/shard_map/fik,fkj->fij/dot_general | solution.py:53
  217.3 7.5 %all-gather.29.cloned.1.call-done = bf16[1280,1280]{1,0:T(8,128)(2,1)} async-done(((bf16[640,1280]{1,0:T(8,128)(2,1)}), bf16[1280,1280]{1,0:T(8,128)(2,1)}) %all-gather.29.cloned.1.call-update) | async-done | bytes 3276816 | tf_op jit(solution)/shard_map/all_gather | solution.py:41
  224.7 15.6 %all-gather.27.cloned.1.call-done = bf16[1280,1280]{1,0:T(8,128)(2,1)} async-done(((bf16[640,1280]{1,0:T(8,128)(2,1)}), bf16[1280,1280]{1,0:T(8,128)(2,1)}) %all-gather.27.cloned.1.call-update) | async-done | bytes 3276816 | tf_op jit(solution)/shard_map/all_gather | solution.py:42
  240.4 7.3 %fusion.7 = bf16[1280,1280]{1,0:T(8,128)(2,1)S(1)} fusion(bf16[1280,1280]{1,0:T(8,128)(2,1)} %all-gather.27.cloned.1.call-done, bf16[1280,1280]{1,0:T(8,128)(2,1)} %all-gather.29.cloned.1.call-done), kind=kOutput, calls=%fused_computation.11 | convolution fusion | flops 4202496000 | bytes 9830400 | tf_op jit(solution)/shard_map/fik,fkj->fij/dot_general | solution.py:45
  247.7 2.3 fusion.15
  250.0 2.5 copy.11
  252.6 0.5 broadcast.81
  253.1 12.1 %reduce.1 = bf16[640,1280]{1,0:T(8,128)(2,1)} reduce(bf16[640,1,1280]{2,1,0:T(2,128)(2,1)S(1)} %bitcast.46, bf16[]{:T(256)} %broadcast.81), dimensions={1}, to_apply=%bitcast.43.reduce_sub_computation | reduce | bytes 3276802
  265.2 3.9 %reshape.220 = bf16[8,2,51200]{2,1,0:T(2,128)(2,1)} reshape(bf16[640,1280]{1,0:T(8,128)(2,1)} %reduce.1) | data formatting | bytes 3276800
  269.1 5.9 %all-to-all-start.1 = ((bf16[8,2,51200]{2,1,0:T(2,128)(2,1)}), bf16[8,2,51200]{2,1,0:T(2,128)(2,1)}, u32[]{:S(2)}, u32[]{:S(2)}) async-start(bf16[8,2,51200]{2,1,0:T(2,128)(2,1)} %reshape.220), calls=%async_computation.1 | async-start | bytes 3276800 | tf_op jit(solution)/shard_map/all_to_all | solution.py:59
  275.0 3.7 fusion.16
  278.7 2.5 copy.10
  281.3 11.9 %reduce = bf16[640,1280]{1,0:T(8,128)(2,1)} reduce(bf16[640,1,1280]{2,1,0:T(2,128)(2,1)S(1)} %bitcast.47, bf16[]{:T(256)} %broadcast.81), dimensions={1}, to_apply=%bitcast.42.reduce_sub_computation | reduce | bytes 3276802
  293.2 3.7 reshape.222
  296.9 16.9 %all-to-all-done.1 = bf16[8,2,51200]{2,1,0:T(2,128)(2,1)} async-done(((bf16[8,2,51200]{2,1,0:T(2,128)(2,1)}), bf16[8,2,51200]{2,1,0:T(2,128)(2,1)}, u32[]{:S(2)}, u32[]{:S(2)}) %all-to-all-start.1) | async-done | bytes 1638432 | tf_op jit(solution)/shard_map/all_to_all | solution.py:59
  313.8 4.3 %all-to-all-start.2 = ((bf16[8,2,51200]{2,1,0:T(2,128)(2,1)}), bf16[8,2,51200]{2,1,0:T(2,128)(2,1)}, u32[]{:S(2)}, u32[]{:S(2)}) async-start(bf16[8,2,51200]{2,1,0:T(2,128)(2,1)} %reshape.222), calls=%async_computation.2 | async-start | bytes 3276800 | tf_op jit(solution)/shard_map/all_to_all | solution.py:60
  318.1 6.4 %reshape.221 = bf16[640,1,1280]{2,1,0:T(2,128)(2,1)} reshape(bf16[8,2,51200]{2,1,0:T(2,128)(2,1)} %all-to-all-done.1) | data formatting | bytes 3276800
  324.5 2.1 copy.6
  326.6 29.5 %all-to-all-done.2 = bf16[8,2,51200]{2,1,0:T(2,128)(2,1)} async-done(((bf16[8,2,51200]{2,1,0:T(2,128)(2,1)}), bf16[8,2,51200]{2,1,0:T(2,128)(2,1)}, u32[]{:S(2)}, u32[]{:S(2)}) %all-to-all-start.2) | async-done | bytes 1638432 | tf_op jit(solution)/shard_map/all_to_all | solution.py:60
  356.2 6.4 %reshape.223 = bf16[640,1,1280]{2,1,0:T(2,128)(2,1)} reshape(bf16[8,2,51200]{2,1,0:T(2,128)(2,1)} %all-to-all-done.2) | data formatting | bytes 3276800
  362.5 2.1 copy.7
  364.7 3.5 broadcast_divide_fusion
  (34 shorter events, 0.5 us)
Async XLA Ops:
  11.6 80.9 %all-to-all-start = ((f32[8,80,1280]{2,1,0:T(8,128)}), f32[8,80,1280]{2,1,0:T(8,128)S(1)}, u32[]{:S(2)}, u32[]{:S(2)}) async-start(f32[8,80,1280]{2,1,0:T(8,128)} %get-tuple-element.3), calls=%async_computation | async-start | bytes 6553600 | tf_op jit(solution)/shard_map/all_to_all | solution.py:33
  18.9 75.8 %all-gather.15.cloned.1.call-start = ((), (), s32[]{:S(2)}) async-start(), calls=%async_computation.3 | async-start | bytes 4915200 | tf_op jit(solution)/shard_map/all_gather | solution.py:42
  20.5 94.6 %all-gather.17.cloned.1.call-start = ((), (), s32[]{:S(2)}) async-start(), calls=%async_computation.4 | async-start | bytes 4915200 | tf_op jit(solution)/shard_map/all_gather | solution.py:41
  94.6 29.6 %copy-start = (bf16[8,80,1280]{2,1,0:T(8,128)(2,1)S(1)}, bf16[8,80,1280]{2,1,0:T(8,128)(2,1)}, u32[]{:S(2)}) copy-start(bf16[8,80,1280]{2,1,0:T(8,128)(2,1)} %divide_convert_fusion) | copy-start | bytes 4915204
  94.6 46.7 %all-gather.21.cloned.1.call-start = ((), (), s32[]{:S(2)}) async-start(), calls=%async_computation.6 | async-start | bytes 4915200 | tf_op jit(solution)/shard_map/all_gather | solution.py:41
  122.4 1.7 copy-start.5
  127.7 29.1 %all-gather.19.cloned.1.call-start = ((), (), s32[]{:S(2)}) async-start(), calls=%async_computation.5 | async-start | bytes 4915200 | tf_op jit(solution)/shard_map/all_gather | solution.py:42
  133.6 32.2 %copy-start.1 = (bf16[640,1280]{1,0:T(8,128)(2,1)S(1)}, bf16[640,1280]{1,0:T(8,128)(2,1)}, u32[]{:S(2)}) copy-start(bf16[640,1280]{1,0:T(8,128)(2,1)} %convolution_convert_fusion.6) | copy-start | bytes 4915204
  133.6 49.4 %all-gather.25.cloned.1.call-start = ((), (), s32[]{:S(2)}) async-start(), calls=%async_computation.8 | async-start | bytes 4915200 | tf_op jit(solution)/shard_map/all_gather | solution.py:41
  164.1 1.7 copy-start.7
  169.4 29.1 %all-gather.23.cloned.1.call-start = ((), (), s32[]{:S(2)}) async-start(), calls=%async_computation.7 | async-start | bytes 4915200 | tf_op jit(solution)/shard_map/all_gather | solution.py:42
  175.3 32.2 %copy-start.2 = (bf16[640,1280]{1,0:T(8,128)(2,1)S(1)}, bf16[640,1280]{1,0:T(8,128)(2,1)}, u32[]{:S(2)}) copy-start(bf16[640,1280]{1,0:T(8,128)(2,1)} %convolution_convert_fusion.5) | copy-start | bytes 4915204
  175.3 49.4 %all-gather.29.cloned.1.call-start = ((), (), s32[]{:S(2)}) async-start(), calls=%async_computation.10 | async-start | bytes 4915200 | tf_op jit(solution)/shard_map/all_gather | solution.py:41
  205.9 1.7 copy-start.8
  211.1 29.3 %all-gather.27.cloned.1.call-start = ((), (), s32[]{:S(2)}) async-start(), calls=%async_computation.9 | async-start | bytes 4915200 | tf_op jit(solution)/shard_map/all_gather | solution.py:42
  217.2 30.5 %copy-start.3 = (bf16[640,1280]{1,0:T(8,128)(2,1)S(1)}, bf16[640,1280]{1,0:T(8,128)(2,1)}, u32[]{:S(2)}) copy-start(bf16[640,1280]{1,0:T(8,128)(2,1)} %convolution_convert_fusion.3) | copy-start | bytes 4915204
  247.7 2.3 copy-start.6
  265.2 9.8 %copy-start.4 = (bf16[1280,1280]{1,0:T(8,128)(2,1)S(1)}, bf16[1280,1280]{1,0:T(8,128)(2,1)}, u32[]{:S(2)}) copy-start(bf16[1280,1280]{1,0:T(8,128)(2,1)} %all-gather.27.cloned.1.call-done) | copy-start | bytes 9830404
  269.1 44.8 %all-to-all-start.1 = ((bf16[8,2,51200]{2,1,0:T(2,128)(2,1)}), bf16[8,2,51200]{2,1,0:T(2,128)(2,1)}, u32[]{:S(2)}, u32[]{:S(2)}) async-start(bf16[8,2,51200]{2,1,0:T(2,128)(2,1)} %reshape.220), calls=%async_computation.1 | async-start | bytes 3276800 | tf_op jit(solution)/shard_map/all_to_all | solution.py:59
  313.8 42.3 %all-to-all-start.2 = ((bf16[8,2,51200]{2,1,0:T(2,128)(2,1)}), bf16[8,2,51200]{2,1,0:T(2,128)(2,1)}, u32[]{:S(2)}, u32[]{:S(2)}) async-start(bf16[8,2,51200]{2,1,0:T(2,128)(2,1)} %reshape.222), calls=%async_computation.2 | async-start | bytes 3276800 | tf_op jit(solution)/shard_map/all_to_all | solution.py:60
Sparse Core Ops, SparseCore 0:
  21.8 13.7 all-gather.14
  94.7 20.3 all-gather.16
  127.8 13.4 all-gather.20
  143.3 13.4 all-gather.18
  169.5 13.4 all-gather.24
  185.0 13.4 all-gather.22
  211.2 13.4 all-gather.28
  226.8 13.4 all-gather.26
